TPU v7x, 512 devices: a whole 4x8x8 slice. The times are simulated.
512 devices in a mesh: elem: 64 (over y, x, core), node: 8 (over z).
Axes of the slice: x: 4, y: 8, z: 8, core: 2. Of those that a mesh axis runs over, the one named last changes fastest.
Arguments:
- factors: bfloat16 [12, 12, 524288], P(None, None, ('elem', 'node')), may hold values from -0.3984375 to 0.3984375
- dest_device: int32 [524288, 1], P(('elem', 'node')), may hold values from 0 to 511; in each aligned block of 1024 rows (0 to 1023, 1024 to 2047, ...) at most 3 rows name the same one
- dest_node: int32 [524288, 1], P(('elem', 'node')), may hold values from 0 to 15
- live_count: int32 [512], P(('elem', 'node')), may hold values from 768 to 1024, as said below
- shift: float32 [12, 8192], P(None, ('elem', 'node')), may hold values from 0.3 to 3
Outputs:
- inverse: float32 [12, 12, 8192], P(None, None, ('elem', 'node'))
Inputs may be any that keep to these rules, and one draw needn't show every extreme that they name: A device's live contributions are its first live_count ones; on some devices all 1024 are live. `dest_device`: among the 1024 contributions of one device, at most 3 name the same owner.
All inputs are finite; a program needn't handle non-finite values.
Results may differ from a plain program's by a relative error of at most 0.0003.
Values sent between devices are 32-bit elements; how exact they have to be, the bound alone decides.
A program may use at most 64 MiB of HBM per device.

v0:
```python
import jax
import jax.numpy as jnp
import numpy as np
from jax import lax
from jax.sharding import PartitionSpec as P


def block_inverse(matrix):
    size = matrix.shape[0]
    lower = [[None] * size for _ in range(size)]
    for column in range(size):
        total = matrix[column, column]
        for inner in range(column):
            total = total - lower[column][inner] * lower[column][inner]
        pivot = jnp.sqrt(total)
        lower[column][column] = pivot
        for target in range(column + 1, size):
            total = matrix[target, column]
            for inner in range(column):
                total = total - lower[target][inner] * lower[column][inner]
            lower[target][column] = total / pivot
    solved = [[None] * size for _ in range(size)]
    for target in range(size):
        solved[target][target] = 1.0 / lower[target][target]
        for column in range(target):
            total = lower[target][column] * solved[column][column]
            for inner in range(column + 1, target):
                total = total + lower[target][inner] * solved[inner][column]
            solved[target][column] = -total / lower[target][target]
    rows_out = []
    for first in range(size):
        entries = []
        for second in range(size):
            total = solved[max(first, second)][first] * solved[max(first, second)][second]
            for inner in range(max(first, second) + 1, size):
                total = total + solved[inner][first] * solved[inner][second]
            entries.append(total)
        rows_out.append(jnp.stack(entries))
    return jnp.stack(rows_out)


def packed_tables(size):
    pairs = [(first, second) for first in range(size) for second in range(first, size)]
    upper_index = np.array([first * size + second for first, second in pairs], np.int32)
    lookup = {}
    for number, pair in enumerate(pairs):
        lookup[pair] = number
    unpack = np.array(
        [
            lookup[min(first, second), max(first, second)]
            for first in range(size)
            for second in range(size)
        ],
        np.int32,
    )
    return (upper_index, unpack)


def shards(factors, dest_device, dest_node, live_count, shift):
    size = factors.shape[0]
    count_local = factors.shape[2]
    node_local = shift.shape[1]
    n_elem = lax.axis_size("elem")
    n_node = lax.axis_size("node")
    devices = n_elem * n_node
    capacity = max(2, 3 * count_local // (2 * devices))
    contrib = jnp.einsum("akc,bkc->abc", factors, factors, preferred_element_type=jnp.float32)
    contrib = contrib.reshape(size * size, count_local)
    upper_index, unpack = packed_tables(size)
    payload = contrib[upper_index]
    owners = dest_device[:, 0]
    alive = jnp.arange(count_local, dtype=jnp.int32) < live_count[0]
    step_rows = min(512, count_local)
    block_count = count_local // step_rows
    strict = (jnp.arange(step_rows)[:, None] > jnp.arange(step_rows)[None, :]).astype(jnp.bfloat16)
    targets = jnp.arange(devices, dtype=jnp.int32)

    def tally(counts, inputs):
        owner_rows, alive_rows = inputs
        member = ((owner_rows[:, None] == targets[None, :]) & alive_rows[:, None]).astype(
            jnp.bfloat16
        )
        before = jnp.dot(strict, member, preferred_element_type=jnp.float32) + counts[None, :]
        ranks = jnp.sum(before * member.astype(jnp.float32), axis=1)
        return (counts + jnp.sum(member.astype(jnp.float32), axis=0), ranks)

    unused, ranks = lax.scan(
        tally,
        jnp.zeros((devices,), jnp.float32),
        (owners.reshape(block_count, step_rows), alive.reshape(block_count, step_rows)),
    )
    ranks = ranks.reshape(count_local).astype(jnp.int32)
    positions = jnp.where(alive, owners * capacity + ranks, devices * capacity)
    width = payload.shape[0]
    outgoing = (
        jnp.zeros((width, devices * capacity), jnp.float32)
        .at[:, positions]
        .set(payload, mode="drop")
    )
    slot_ids = (
        jnp.full((1, devices * capacity), -1, jnp.int32)
        .at[0, positions]
        .set(dest_node[:, 0], mode="drop")
    )
    outgoing = outgoing.reshape(width, n_elem, n_node, capacity)
    slot_ids = slot_ids.reshape(1, n_elem, n_node, capacity)
    sectioned = (
        lax.all_to_all(outgoing, "elem", split_axis=1, concat_axis=1, tiled=True),
        lax.all_to_all(slot_ids, "elem", split_axis=1, concat_axis=1, tiled=True),
    )
    arrived = (
        lax.all_to_all(sectioned[0], "node", split_axis=2, concat_axis=2, tiled=True),
        lax.all_to_all(sectioned[1], "node", split_axis=2, concat_axis=2, tiled=True),
    )
    received = arrived[0].reshape(width, devices * capacity)
    received_ids = arrived[1].reshape(devices * capacity)
    selector = (received_ids[:, None] == jnp.arange(node_local, dtype=jnp.int32)[None, :]).astype(
        jnp.float32
    )
    assembled = jnp.dot(
        received, selector, precision=lax.Precision.HIGHEST, preferred_element_type=jnp.float32
    )
    assembled = assembled[unpack]
    assembled = assembled.reshape(size, size, node_local)
    identity = jnp.eye(size, dtype=jnp.float32)
    matrix = assembled + identity[:, :, None] * shift[:, None, :]
    return block_inverse(matrix)


def solution(mesh):
    placed = (
        P(None, None, ("elem", "node")),
        P(("elem", "node"), None),
        P(("elem", "node"), None),
        P(("elem", "node")),
        P(None, ("elem", "node")),
    )
    return jax.shard_map(
        shards,
        mesh=mesh,
        in_specs=placed,
        out_specs=P(None, None, ("elem", "node")),
        check_vma=False,
    )
```

profile of v0, /device:TPU:1, one launch (start us, length us, event | category | flops | bytes accessed | tf_op | source)
XLA Modules:
  0.0 128.6 jit_solution(1012045936611732019)
XLA Ops:
  0.0 0.5 broadcast.766
  0.5 1.2 reduce.9
  2.5 2.0 %while.13 = (s32[]{:T(128)}, f32[512]{0:T(512)S(1)}, f32[2,512]{1,0:T(2,128)S(1)}, s32[2,512]{1,0:T(2,128)S(1)}, pred[2,512]{1,0:T(4,128)(4,1)S(1)}, /*index=5*/s32[]{:T(128)}, s32[]{:T(128)}) while((s32[]{:T(128)}, f32[512]{0:T(512)S(1)}, f32[2,512]{1,0:T(2,128)S(1)}, s32[2,512]{1,0:T(2,128)S(1)}, pred[2,512]{1,0:T(4,128)(4,1)S(1)}, ...), condition=%wide.region_3.4_spmd.clone, body=%wide.region_0.3_spmd.clone.sunk | while | flops 272629760 | bytes 28779 | solution.py:87
  2.5 0.3 convert_reduce_fusion.2
  2.8 0.6 fusion.421
  3.5 0.3 convert_reduce_fusion.2
  3.8 0.6 fusion.421
  4.5 0.1 and_reduce_fusion
  4.6 0.1 fusion.18
  4.7 4.5 %scatter_custom_fusion.1 = s32[1536]{0:T(1024)S(1)} fusion(s32[1024]{0:T(1024)S(1)} %broadcast_select_fusion.1, s32[1024]{0:T(1024)} %bitcast.721, s32[]{:T(128)} %constant.27.clone.1), kind=kCustom, calls=%fused_computation.49 | custom fusion | bytes 6656
  9.2 0.2 reshape.30685
  9.4 1.1 copy.48
  10.5 11.6 %all-to-all-start.2 = ((s32[1,64,8,3]{2,0,3,1:T(1,128)}), s32[1,64,8,3]{2,0,3,1:T(1,128)S(1)}, u32[]{:S(2)}, u32[]{:S(2)}) async-start(s32[1,64,8,3]{2,0,3,1:T(1,128)} %copy.48), calls=%async_computation.2 | async-start | bytes 196608 | tf_op jit(solution)/shard_map/all_to_all | solution.py:109
  22.1 4.9 %copy.41 = bf16[12,12,1024]{1,0,2:T(8,128)(2,1)} copy(bf16[12,12,1024]{2,1,0:T(8,128)(2,1)S(1)} %copy-done) | data formatting | bytes 589824 | tf_op args[0]
  27.0 9.0 %convolution_bitcast_fusion = f32[12,12,1024]{0,1,2:T(8,128)} fusion(bf16[12,12,1024]{1,0,2:T(8,128)(2,1)} %copy.41), kind=kOutput, calls=%fused_computation.21 | convolution fusion | flops 3538944 | bytes 884736 | tf_op jit(solution)/shard_map/akc,bkc->abc/dot_general | solution.py:67
  36.0 5.3 %copy.43 = f32[12,12,1024]{2,1,0:T(8,128)S(1)} copy(f32[12,12,1024]{0,1,2:T(8,128)} %convolution_bitcast_fusion) | data formatting | bytes 1179648 | tf_op jit(solution)/shard_map/akc,bkc->abc/transpose | solution.py:67
  41.4 0.7 gather_fusion
  42.1 0.2 copy.44
  42.3 3.3 %scatter_custom_fusion = f32[78,1536]{0,1:T(8,128)S(1)} fusion(s32[1024]{0:T(1024)S(1)} %bitcast.719, f32[1024,78]{1,0:T(8,128)S(1)} %copy.44, f32[]{:T(128)} %constant.21.clone.1), kind=kCustom, calls=%fused_computation.25 | custom fusion | bytes 479236 | tf_op jit(solution)/shard_map/scatter | solution.py:98
  45.6 0.3 reshape.30683
  46.0 1.0 copy.45
  46.9 10.3 %all-to-all-start = ((f32[78,64,8,3]{0,2,3,1:T(8,128)}), f32[78,64,8,3]{0,2,3,1:T(8,128)S(1)}, u32[]{:S(2)}, u32[]{:S(2)}) async-start(f32[78,64,8,3]{0,2,3,1:T(8,128)} %copy.45), calls=%async_computation | async-start | bytes 1572864 | tf_op jit(solution)/shard_map/all_to_all | solution.py:108
  57.2 0.1 copy.49
  57.3 0.6 broadcast.802
  57.9 0.7 reduce.10
  58.6 0.7 reshape.31217
  59.2 21.0 %all-to-all-done = f32[78,64,8,3]{0,2,3,1:T(8,128)S(1)} async-done(((f32[78,64,8,3]{0,2,3,1:T(8,128)}), f32[78,64,8,3]{0,2,3,1:T(8,128)S(1)}, u32[]{:S(2)}, u32[]{:S(2)}) %all-to-all-start) | async-done | bytes 479264 | tf_op jit(solution)/shard_map/all_to_all | solution.py:108
  80.2 10.0 %all-to-all-start.3 = ((s32[8,1,192]{2,1,0:T(1,128)}), s32[8,1,192]{2,1,0:T(1,128)S(1)}, u32[]{:S(2)}, u32[]{:S(2)}) async-start(s32[8,1,192]{2,1,0:T(1,128)} %reshape.31217), calls=%async_computation.3 | async-start | bytes 16384 | tf_op jit(solution)/shard_map/all_to_all | solution.py:113
  90.3 1.0 copy.46
  91.3 5.5 %all-to-all-done.3 = s32[8,1,192]{2,1,0:T(1,128)S(1)} async-done(((s32[8,1,192]{2,1,0:T(1,128)}), s32[8,1,192]{2,1,0:T(1,128)S(1)}, u32[]{:S(2)}, u32[]{:S(2)}) %all-to-all-start.3) | async-done | bytes 6176 | tf_op jit(solution)/shard_map/all_to_all | solution.py:113
  96.9 3.7 %all-to-all-start.1 = ((f32[78,64,8,3]{0,1,3,2:T(8,128)}), f32[78,64,8,3]{0,1,3,2:T(8,128)S(1)}, u32[]{:S(2)}, u32[]{:S(2)}) async-start(f32[78,64,8,3]{0,1,3,2:T(8,128)} %copy.46), calls=%async_computation.1 | async-start | bytes 1572864 | tf_op jit(solution)/shard_map/all_to_all | solution.py:112
  100.6 0.7 reduce.11
  101.3 0.1 reshape.31218
  101.4 0.2 copy.50
  101.5 0.2 eq.37
  101.7 20.6 %all-to-all-done.1 = f32[78,64,8,3]{0,1,3,2:T(8,128)S(1)} async-done(((f32[78,64,8,3]{0,1,3,2:T(8,128)}), f32[78,64,8,3]{0,1,3,2:T(8,128)S(1)}, u32[]{:S(2)}, u32[]{:S(2)}) %all-to-all-start.1) | async-done | bytes 479264 | tf_op jit(solution)/shard_map/all_to_all | solution.py:112
  122.4 0.5 copy.47
  122.9 0.4 reshape.30684
  123.3 1.0 fusion.14
  124.3 0.7 gather_fusion.1
  125.0 0.1 multiply_add_fusion
  125.1 0.2 rsqrt_multiply_fusion
  125.6 0.1 fusion.396
  125.6 0.1 fusion.399
  125.7 0.1 fusion.403
  125.8 0.1 fusion.407
  127.4 0.6 copy-done.4
  128.0 0.6 constant_dynamic-update-slice_fusion
  (91 shorter events, 1.8 us)
Async XLA Ops:
  2.4 2.0 %copy-start.1 = (s32[1024,1]{0,1:T(1,128)S(1)}, s32[1024,1]{0,1:T(1,128)}, u32[]{:S(2)}) copy-start(s32[1024,1]{0,1:T(1,128)} %param.12) | copy-start | bytes 12292
  2.4 2.1 %copy-start.7 = (s32[2]{0:T(128)S(1)}, s32[2]{0:T(128)}, u32[]{:S(2)}) copy-start(s32[2]{0:T(128)} %constant.54) | copy-start | bytes 28
  2.4 2.2 %copy-start.6 = (s32[2]{0:T(128)S(1)}, s32[2]{0:T(128)}, u32[]{:S(2)}) copy-start(s32[2]{0:T(128)} %constant.51) | copy-start | bytes 28
  2.4 19.6 %copy-start = (bf16[12,12,1024]{2,1,0:T(8,128)(2,1)S(1)}, bf16[12,12,1024]{2,1,0:T(8,128)(2,1)}, u32[]{:S(2)}) copy-start(bf16[12,12,1024]{2,1,0:T(8,128)(2,1)} %param.11) | copy-start | bytes 884740
  10.5 36.5 %all-to-all-start.2 = ((s32[1,64,8,3]{2,0,3,1:T(1,128)}), s32[1,64,8,3]{2,0,3,1:T(1,128)S(1)}, u32[]{:S(2)}, u32[]{:S(2)}) async-start(s32[1,64,8,3]{2,0,3,1:T(1,128)} %copy.48), calls=%async_computation.2 | async-start | bytes 196608 | tf_op jit(solution)/shard_map/all_to_all | solution.py:109
  27.0 9.0 %copy-start.3 = (s32[144]{0:T(256)S(1)}, s32[144]{0:T(256)}, u32[]{:S(2)}) copy-start(s32[144]{0:T(256)} %constant.62) | copy-start | bytes 1732
  27.0 9.0 %copy-start.5 = (s32[78]{0:T(128)S(1)}, s32[78]{0:T(128)}, u32[]{:S(2)}) copy-start(s32[78]{0:T(128)} %constant.61) | copy-start | bytes 940
  46.9 33.3 %all-to-all-start = ((f32[78,64,8,3]{0,2,3,1:T(8,128)}), f32[78,64,8,3]{0,2,3,1:T(8,128)S(1)}, u32[]{:S(2)}, u32[]{:S(2)}) async-start(f32[78,64,8,3]{0,2,3,1:T(8,128)} %copy.45), calls=%async_computation | async-start | bytes 1572864 | tf_op jit(solution)/shard_map/all_to_all | solution.py:108
  80.2 16.6 %all-to-all-start.3 = ((s32[8,1,192]{2,1,0:T(1,128)}), s32[8,1,192]{2,1,0:T(1,128)S(1)}, u32[]{:S(2)}, u32[]{:S(2)}) async-start(s32[8,1,192]{2,1,0:T(1,128)} %reshape.31217), calls=%async_computation.3 | async-start | bytes 16384 | tf_op jit(solution)/shard_map/all_to_all | solution.py:113
  90.3 34.7 %copy-start.2 = (f32[12,16]{1,0:T(8,128)S(1)}, f32[12,16]{1,0:T(8,128)}, u32[]{:S(2)}) copy-start(f32[12,16]{1,0:T(8,128)} %param.15) | copy-start | bytes 2308
  96.9 25.5 %all-to-all-start.1 = ((f32[78,64,8,3]{0,1,3,2:T(8,128)}), f32[78,64,8,3]{0,1,3,2:T(8,128)S(1)}, u32[]{:S(2)}, u32[]{:S(2)}) async-start(f32[78,64,8,3]{0,1,3,2:T(8,128)} %copy.46), calls=%async_computation.1 | async-start | bytes 1572864 | tf_op jit(solution)/shard_map/all_to_all | solution.py:112
  127.4 0.6 copy-start.4
where the time goes:
time: 129 us
  waiting for transfers between devices  47.1 us (37%)
  starting transfers between devices  35.7 us (28%)
  local copies, waits for them, and re-layouts  28.5 us (22%)
  matrix products  11.2 us (9%)
  other arithmetic  4.87 us (4%)
    all_to_all x1, waiting for transfers between devices, shards(): lax.all_to_all(outgoing, 'elem', split_axis=1, concat_axis=1, tiled=True)  21 us
    all_to_all x1, waiting for transfers between devices, shards(): lax.all_to_all(sectioned[0], 'node', split_axis=2, concat_axis=2, tiled=T...  20.6 us
    unnamed x34, local copies, waits for them, and re-layouts  11.9 us
    all_to_all x1, starting transfers between devices, shards(): lax.all_to_all(slot_ids, 'elem', split_axis=1, concat_axis=1, tiled=True)  11.6 us
    all_to_all x1, starting transfers between devices, shards(): lax.all_to_all(outgoing, 'elem', split_axis=1, concat_axis=1, tiled=True)  10.3 us
    all_to_all x1, starting transfers between devices, shards(): lax.all_to_all(sectioned[1], 'node', split_axis=2, concat_axis=2, tiled=T...  10 us
    dot_general x1, matrix products, shards(): jnp.einsum('akc,bkc->abc', factors, factors, preferred_element_type=jnp.f...  8.99 us
    all_to_all x1, waiting for transfers between devices, shards(): lax.all_to_all(sectioned[1], 'node', split_axis=2, concat_axis=2, tiled=T...  5.53 us
  transfers between devices with their start and end apart: 4, of which 3 were waited for; matrix products, arithmetic and copies ran while one was open for 23% of the time, Pallas kernels for 0%

commit v1 on v0

v1 whole, which is shorter than its diff:
```python
import functools

import jax
import jax.numpy as jnp
from jax import lax
from jax.experimental import pallas as pl
from jax.experimental.pallas import tpu as pltpu
from jax.sharding import PartitionSpec as P

MESH = pl.DeviceIdType.MESH
F32 = jnp.float32
BF16 = jnp.bfloat16
SIZE = 12
COUNT = 1024
NODES = 16
NX, NY, NZ, NC = 4, 8, 8, 2
OFFSET = [a * SIZE - a * (a - 1) // 2 for a in range(SIZE)]
ROWS = 80
MESSAGE = 120


def lanes(shape):
    return lax.broadcasted_iota(jnp.int32, shape, len(shape) - 1)


def ranks_of(owner):
    counts = [jnp.zeros((8, 128), F32) for _ in range(8)]
    rows = [owner[:, b * 128 : (b + 1) * 128] for b in range(8)]
    before = lax.broadcasted_iota(jnp.int32, (128, 128), 0) < lanes((128, 128))
    for b in range(8):
        column = jnp.broadcast_to(rows[b], (128, 128)).T
        for later in range(b, 8):
            same = column == rows[later]
            if later == b:
                same = same & before
            hits = jnp.where(same, 1.0, 0.0)
            counts[later] = counts[later] + jnp.sum(hits.reshape(16, 8, 128), axis=0)
    return jnp.concatenate([jnp.sum(c, axis=0, keepdims=True) for c in counts], axis=1)


def exchange_kernel(
    factors,
    owner_ref,
    node_ref,
    live_ref,
    out,
    lhs,
    routed,
    packed,
    send1,
    recv1,
    dense,
    recv2,
    send3,
    recv3,
    ssem1,
    rsem1,
    ssem2,
    rsem2,
    ssem3,
    rsem3,
):
    elem = lax.axis_index("elem")
    z = lax.axis_index("node")
    core = lax.rem(elem, NC)
    x = lax.rem(elem // NC, NX)
    y = elem // (NC * NX)

    def device(y_at, x_at, core_at, z_at):
        return ((y_at * NX + x_at) * NC + core_at, z_at)

    def partner1(i):
        return device(y, lax.rem(x + i // 2, NX), lax.rem(core + i, NC), z)

    def partner2(i):
        return device(lax.rem(y + i * (1 - core), NY), x, core, lax.rem(z + i * core, NZ))

    def partner3(i):
        return device(lax.rem(y + i * core, NY), x, core, lax.rem(z + i * (1 - core), NZ))

    barrier = pltpu.get_barrier_semaphore()
    for partner in (partner1, partner2, partner3):
        for i in range(1, 8):
            pl.semaphore_signal(barrier, inc=1, device_id=partner(i), device_id_type=MESH)

    first = y * (1 - core) + z * core
    second = z * (1 - core) + y * core

    for a in range(SIZE):
        lhs[a * 16 : a * 16 + SIZE, :] = factors[a]
    lhs[192:208, :] = jnp.broadcast_to(node_ref[...].astype(F32), (16, COUNT)).astype(BF16)

    owner = owner_ref[...]
    rank = ranks_of(owner.astype(F32)).astype(jnp.int32)
    owner_z = owner & 7
    owner_core = (owner >> 3) & 1
    owner_x = (owner >> 4) & 3
    owner_y = owner >> 6
    other = owner_core ^ core
    step = (owner_x - x + NX) & 3
    slot = jnp.where(rank < 2, other * 128 + rank * 64, 256 + other * 64)
    slot = slot + step * 384 + owner_y * 8 + owner_z
    slot = jnp.where(lanes((1, COUNT)) < live_ref[0], slot, -1)

    low = lanes((40, 128)) < 64

    def prepare(step):
        wanted = lax.broadcasted_iota(jnp.int32, (384, COUNT), 0)
        choice = jnp.where(wanted == slot - step * 384, 1.0, 0.0).astype(BF16)
        result = lax.dot_general(
            lhs[...], choice, (((1,), (1,)), ((), ())), preferred_element_type=F32
        )
        for t in range(3):
            routed[t] = result[:, t * 128 : (t + 1) * 128]

        def product(t, carry):
            total = [None] * SIZE
            for k in range(SIZE):
                column = routed[t, pl.ds(k, SIZE, stride=16), :]
                for a in range(SIZE):
                    term = routed[t, a * 16 + k : a * 16 + k + 1, :] * column
                    total[a] = term if k == 0 else total[a] + term
            for a in range(SIZE):
                packed[t, OFFSET[a] : OFFSET[a] + SIZE - a, :] = total[a][a:SIZE]
            packed[t, 78:80, :] = routed[t, 192:194, :]
            return carry

        lax.fori_loop(0, 3, product, 0)
        upper, bottom = packed[2, 0:40, :], packed[2, 40:80, :]
        first_half = jnp.where(low, upper, pltpu.roll(bottom, 64, 1))
        second_half = jnp.where(low, pltpu.roll(upper, 64, 1), bottom)
        return first_half, second_half

    def fill(target, index, part, half):
        target[index, 0:ROWS, :] = packed[part]
        target[index, ROWS:MESSAGE, :] = half

    def copy1(i):
        return pltpu.make_async_remote_copy(
            src_ref=send1.at[i],
            dst_ref=recv1.at[i],
            send_sem=ssem1.at[i],
            recv_sem=rsem1.at[i],
            device_id=partner1(i),
            device_id_type=MESH,
        )

    pl.semaphore_wait(barrier, 21)

    def pair(step, carry):
        first_half, second_half = prepare(step)
        fill(send1, 2 * step, 0, first_half)
        fill(send1, 2 * step + 1, 1, second_half)
        copy1(2 * step).start()
        copy1(2 * step + 1).start()
        return carry

    lax.fori_loop(1, NX, pair, 0)
    first_half, second_half = prepare(0)
    fill(send1, 1, 1, second_half)
    copy1(1).start()
    fill(recv1, 0, 0, first_half)

    lane = lanes((1, 256)) & 63
    lane_y, lane_z = lane >> 3, lane & 7
    base = (lane_y * (1 - core) + lane_z * core) * 128
    base = base + (lane_z * (1 - core) + lane_y * core) * 16
    low_row = lanes((1, 128)) < 64

    def gather(i):
        top = recv1[i, 0:ROWS, :]
        half = recv1[i, ROWS:MESSAGE, :]
        ids_half = recv1[i, ROWS + 38 : ROWS + 39, :]
        ids = jnp.concatenate(
            [recv1[i, 78:79, :], jnp.where(low_row, pltpu.roll(ids_half, 64, 1), ids_half)], axis=1
        )
        place = base + ids.astype(jnp.int32)
        spread = jnp.concatenate([jnp.where(low, half, 0.0), jnp.where(low, 0.0, half)], axis=0)
        values = jnp.concatenate([top, spread], axis=1)
        high = values.astype(BF16)
        rest = values - high.astype(F32)
        middle = rest.astype(BF16)
        tail = (rest - middle.astype(F32)).astype(BF16)
        pieces = jnp.concatenate([high, middle, tail], axis=0)
        for part in range(4):
            wanted = lax.broadcasted_iota(jnp.int32, (256, 256), 0) + part * 256
            choice = jnp.where(wanted == place, 1.0, 0.0).astype(BF16)
            found = lax.dot_general(
                pieces, choice, (((1,), (1,)), ((), ())), preferred_element_type=F32
            )
            found = found[0:ROWS] + found[ROWS : 2 * ROWS] + found[2 * ROWS : 3 * ROWS]
            yield part, found

    for part, found in gather(0):
        dense[2 * part] = found[:, 0:128]
        dense[2 * part + 1] = found[:, 128:256]

    def absorb(i, carry):
        copy1(i).wait_recv()
        for part, found in gather(i):
            dense[2 * part] = dense[2 * part] + found[:, 0:128]
            dense[2 * part + 1] = dense[2 * part + 1] + found[:, 128:256]
        return carry

    lax.fori_loop(1, 8, absorb, 0)

    def copy2(i):
        return pltpu.make_async_remote_copy(
            src_ref=dense.at[lax.rem(first + i, 8)],
            dst_ref=recv2.at[i],
            send_sem=ssem2.at[i],
            recv_sem=rsem2.at[i],
            device_id=partner2(i),
            device_id_type=MESH,
        )

    for i in (4, 3, 5, 2, 6, 1, 7):
        copy2(i).start()
    total = dense[first]
    for i in (1, 7, 2, 6, 3, 5, 4):
        copy2(i).wait_recv()
        total = total + recv2[i]

    lane_full = lanes((8, 128))

    def swap(tiles):
        for span in (4, 2, 1):
            width = span * 16
            lower = (lane_full & width) == 0
            result = list(tiles)
            for v in range(8):
                if v & span:
                    continue
                one, two = tiles[v], tiles[v + span]
                result[v] = jnp.where(lower, one, pltpu.roll(two, width, 1))
                result[v + span] = jnp.where(lower, pltpu.roll(one, 128 - width, 1), two)
            tiles = result
        return tiles

    rows = [total[v * 8 : v * 8 + 8] for v in range(10)]
    empty = jnp.zeros((8, 128), F32)
    main = swap(rows[0:8])
    extra = swap(rows[8:10] + [empty] * 6)
    for q in range(8):
        send3[q, 0:8, :] = main[q]
        send3[q, 8:16, :] = extra[q]

    def copy3(i):
        return pltpu.make_async_remote_copy(
            src_ref=send3.at[lax.rem(second + i, 8)],
            dst_ref=recv3.at[i],
            send_sem=ssem3.at[i],
            recv_sem=rsem3.at[i],
            device_id=partner3(i),
            device_id_type=MESH,
        )

    for i in (4, 3, 5, 2, 6, 1, 7):
        copy3(i).start()
    result = send3[second]
    for i in (1, 7, 2, 6, 3, 5, 4):
        copy3(i).wait_recv()
        result = result + recv3[i]
    out[...] = result
    for i in range(1, 8):
        copy1(i).wait_send()
        copy2(i).wait_send()
        copy3(i).wait_send()


def inverse_kernel(sums, shift, out, flat, square):
    for v in range(10):
        source = sums[0:8, :] if v < 8 else sums[8:16, :]
        turned = 16 * v % 128
        flat[v * 8 : v * 8 + 8, :] = pltpu.roll(source, 128 - turned, 1) if turned else source
    for j in range(SIZE):
        square[j, j:SIZE, :] = flat[OFFSET[j] : OFFSET[j] + SIZE - j, 0:NODES]
        for i in range(j):
            place = OFFSET[i] + j - i
            square[j, i : i + 1, :] = flat[place : place + 1, 0:NODES]
    row = lax.broadcasted_iota(jnp.int32, (SIZE, NODES), 0)
    columns = []
    for j in range(SIZE):
        added = jnp.where(row == j, shift[j : j + 1, :], 0.0)
        columns.append(square[j] + added)
    for j in range(SIZE):
        current = columns[j]
        here = row == j
        scale = 1.0 / current[j : j + 1, :]
        scaled = jnp.where(here, -scale, current * scale)
        for k in range(SIZE):
            if k == j:
                continue
            kept = jnp.where(here, 0.0, columns[k])
            columns[k] = kept - scaled * current[k : k + 1, :]
        columns[j] = scaled
    for j in range(SIZE):
        out[j] = -columns[j]


def shards(factors, dest_device, dest_node, live_count, shift):
    vmem = pl.BlockSpec(memory_space=pltpu.VMEM)
    sums = pl.pallas_call(
        exchange_kernel,
        out_shape=jax.ShapeDtypeStruct((16, 128), F32),
        in_specs=[vmem, vmem, vmem, pl.BlockSpec(memory_space=pltpu.SMEM)],
        out_specs=vmem,
        scratch_shapes=[
            pltpu.VMEM((208, COUNT), BF16),
            pltpu.VMEM((3, 208, 128), F32),
            pltpu.VMEM((3, ROWS, 128), F32),
            pltpu.VMEM((8, MESSAGE, 128), F32),
            pltpu.VMEM((8, MESSAGE, 128), F32),
            pltpu.VMEM((8, ROWS, 128), F32),
            pltpu.VMEM((8, ROWS, 128), F32),
            pltpu.VMEM((8, 16, 128), F32),
            pltpu.VMEM((8, 16, 128), F32),
        ]
        + [pltpu.SemaphoreType.DMA((8,))] * 6,
        compiler_params=pltpu.CompilerParams(collective_id=0, has_side_effects=True),
    )(factors, dest_device.reshape(1, COUNT), dest_node.reshape(1, COUNT), live_count)
    return pl.pallas_call(
        inverse_kernel,
        out_shape=jax.ShapeDtypeStruct((SIZE, SIZE, NODES), F32),
        in_specs=[vmem, vmem],
        out_specs=vmem,
        scratch_shapes=[pltpu.VMEM((ROWS, 128), F32), pltpu.VMEM((SIZE, SIZE, NODES), F32)],
    )(sums, shift)


def solution(mesh):
    placed = (
        P(None, None, ("elem", "node")),
        P(("elem", "node"), None),
        P(("elem", "node"), None),
        P(("elem", "node")),
        P(None, ("elem", "node")),
    )
    return jax.shard_map(
        shards,
        mesh=mesh,
        in_specs=placed,
        out_specs=P(None, None, ("elem", "node")),
        check_vma=False,
    )
```

time: 129 us -> 39.2 us (0.30)
  waiting for transfers between devices: 47.1 us -> 0 us
  Pallas kernels: 0 us -> 38.3 us
  starting transfers between devices: 35.7 us -> 0 us
  local copies, waits for them, and re-layouts: 28.5 us -> 0 us
  matrix products: 11.2 us -> 0 us
  other arithmetic: 4.87 us -> 0 us
    all_to_all x4 -> x0, waiting for transfers between devices: 47.1 us -> none  [the longest x1 21 us: shards(): lax.all_to_all(outgoing, 'elem', split_axis=1, concat_axis=1, tiled=True)]
    pallas_call x0 -> x2, Pallas kernels: none -> 38.3 us  [the longest x1 36.7 us: shards(): pl.pallas_call(exchange_kernel, out_shape=jax.ShapeDtypeStruct((16, 128),...]
    all_to_all x4 -> x0, starting transfers between devices: 35.7 us -> none  [the longest x1 11.6 us: shards(): lax.all_to_all(slot_ids, 'elem', split_axis=1, concat_axis=1, tiled=True)]
    unnamed x34 -> x0, local copies, waits for them, and re-layouts: 11.9 us -> none
    dot_general x4 -> x0, matrix products: 11.2 us -> none  [the longest x1 8.99 us: shards(): jnp.einsum('akc,bkc->abc', factors, factors, preferred_element_type=jnp.f...]
    transpose x1 -> x0, local copies, waits for them, and re-layouts: 5.31 us -> none  [shards(): jnp.einsum('akc,bkc->abc', factors, factors, preferred_element_type=jnp.f...]
    scatter x1 -> x0, local copies, waits for them, and re-layouts: 3.28 us -> none  [shards(): outgoing = jnp.zeros((width, devices * capacity), jnp.float32).at[:, posi...]
    reshape x7 -> x0, local copies, waits for them, and re-layouts: 3.03 us -> none  [the longest x2 1.31 us: shards(): outgoing = outgoing.reshape(width, n_elem, n_node, capacity)]
  transfers between devices with their start and end apart: 4 -> 0, of which waited for: 3 -> 0; matrix products, arithmetic and copies ran while one was open for 23% -> 0% of each run, Pallas kernels for 0% -> 0%
where the time goes in v1:
time: 39.2 us; the launch traced here: 39 us
  Pallas kernels  38.3 us (98%)
  between operations  0.66 us (2%)
    pallas_call x1, Pallas kernels, shards(): pl.pallas_call(exchange_kernel, out_shape=jax.ShapeDtypeStruct((16, 128),...  36.7 us
    pallas_call x1, Pallas kernels, shards(): pl.pallas_call(inverse_kernel, out_shape=jax.ShapeDtypeStruct((SIZE, SIZE...  1.62 us

profile of v1, /device:TPU:1, one launch (start us, length us, event | category | flops | bytes accessed | tf_op | source)
XLA Modules:
  0.0 39.0 jit_solution(14335538220312348516)
XLA Ops:
  0.7 36.7 %shard_map.55.sums = f32[16,128]{1,0:T(8,128)} custom-call(bf16[12,12,1024]{2,1,0:T(8,128)(2,1)} %factors.1, s32[1,1024]{1,0:T(1,128)} %bitcast.2, s32[1,1024]{1,0:T(1,128)} %bitcast.3, s32[1]{0:T(128)S(6)} %copy.6.live_ref), custom_call_target="tpu_custom_call" | custom-call | tf_op jit(solution)/shard_map/pallas_call | solution.py:303
  37.4 1.6 %shard_map.56 = f32[12,12,16]{2,1,0:T(8,128)} custom-call(f32[16,128]{1,0:T(8,128)} %shard_map.55.sums, f32[12,16]{1,0:T(8,128)} %shift.1), custom_call_target="tpu_custom_call" | custom-call | tf_op jit(solution)/shard_map/pallas_call | solution.py:322

commit v2 on v1

--- a/solution.py
+++ b/solution.py
@@ -39,11 +39,15 @@
 
 
 def exchange_kernel(
+    factors_in,
+    owner_in,
+    node_in,
+    live_ref,
+    out,
     factors,
     owner_ref,
     node_ref,
-    live_ref,
-    out,
+    isem,
     lhs,
     routed,
     packed,
@@ -60,6 +64,14 @@
     ssem3,
     rsem3,
 ):
+    inputs = [
+        pltpu.make_async_copy(source, target, isem.at[n])
+        for n, (source, target) in enumerate(
+            [(owner_in, owner_ref), (node_in, node_ref), (factors_in, factors)]
+        )
+    ]
+    for copy in inputs:
+        copy.start()
     elem = lax.axis_index("elem")
     z = lax.axis_index("node")
     core = lax.rem(elem, NC)
@@ -86,10 +98,7 @@
     first = y * (1 - core) + z * core
     second = z * (1 - core) + y * core
 
-    for a in range(SIZE):
-        lhs[a * 16 : a * 16 + SIZE, :] = factors[a]
-    lhs[192:208, :] = jnp.broadcast_to(node_ref[...].astype(F32), (16, COUNT)).astype(BF16)
-
+    inputs[0].wait()
     owner = owner_ref[...]
     rank = ranks_of(owner.astype(F32)).astype(jnp.int32)
     owner_z = owner & 7
@@ -99,8 +108,17 @@
     other = owner_core ^ core
     step = (owner_x - x + NX) & 3
     slot = jnp.where(rank < 2, other * 128 + rank * 64, 256 + other * 64)
-    slot = slot + step * 384 + owner_y * 8 + owner_z
+    outer = owner_y * (1 - owner_core) + owner_z * owner_core
+    inner = owner_z * (1 - owner_core) + owner_y * owner_core
+    lane = (outer * 8 + inner + ((2 * step + other) & 3) * 16) & 63
+    slot = slot + step * 384 + lane
     slot = jnp.where(lanes((1, COUNT)) < live_ref[0], slot, -1)
+
+    inputs[1].wait()
+    inputs[2].wait()
+    for a in range(SIZE):
+        lhs[a * 16 : a * 16 + SIZE, :] = factors[a]
+    lhs[192:208, :] = jnp.broadcast_to(node_ref[...].astype(F32), (16, COUNT)).astype(BF16)
 
     low = lanes((40, 128)) < 64
 
@@ -145,64 +163,75 @@
             device_id_type=MESH,
         )
 
-    pl.semaphore_wait(barrier, 21)
-
-    def pair(step, carry):
+    def send(step):
         first_half, second_half = prepare(step)
         fill(send1, 2 * step, 0, first_half)
         fill(send1, 2 * step + 1, 1, second_half)
+
+    def start(step):
         copy1(2 * step).start()
         copy1(2 * step + 1).start()
+
+    send(2)
+    pl.semaphore_wait(barrier, 21)
+    start(2)
+
+    def pair(turn, carry):
+        step = 1 + 2 * turn
+        send(step)
+        start(step)
         return carry
 
-    lax.fori_loop(1, NX, pair, 0)
+    lax.fori_loop(0, 2, pair, 0)
     first_half, second_half = prepare(0)
     fill(send1, 1, 1, second_half)
     copy1(1).start()
     fill(recv1, 0, 0, first_half)
 
-    lane = lanes((1, 256)) & 63
-    lane_y, lane_z = lane >> 3, lane & 7
-    base = (lane_y * (1 - core) + lane_z * core) * 128
-    base = base + (lane_z * (1 - core) + lane_y * core) * 16
+    base = (lanes((1, 256)) & 15) * 16
+    block = (lanes((1, 256)) & 63) >> 4
     low_row = lanes((1, 128)) < 64
-
-    def gather(i):
-        top = recv1[i, 0:ROWS, :]
-        half = recv1[i, ROWS:MESSAGE, :]
-        ids_half = recv1[i, ROWS + 38 : ROWS + 39, :]
-        ids = jnp.concatenate(
-            [recv1[i, 78:79, :], jnp.where(low_row, pltpu.roll(ids_half, 64, 1), ids_half)], axis=1
-        )
-        place = base + ids.astype(jnp.int32)
-        spread = jnp.concatenate([jnp.where(low, half, 0.0), jnp.where(low, 0.0, half)], axis=0)
-        values = jnp.concatenate([top, spread], axis=1)
-        high = values.astype(BF16)
-        rest = values - high.astype(F32)
-        middle = rest.astype(BF16)
-        tail = (rest - middle.astype(F32)).astype(BF16)
-        pieces = jnp.concatenate([high, middle, tail], axis=0)
+    wanted = lax.broadcasted_iota(jnp.int32, (256, 256), 0)
+
+    def batch(begin):
         for part in range(4):
-            wanted = lax.broadcasted_iota(jnp.int32, (256, 256), 0) + part * 256
+            values = ids = None
+            for source in range(4):
+                i = begin + source
+                half = recv1[i, ROWS:MESSAGE, :]
+                spread = jnp.concatenate(
+                    [jnp.where(low, half, 0.0), jnp.where(low, 0.0, half)], axis=0
+                )
+                value = jnp.concatenate([recv1[i, 0:ROWS, :], spread], axis=1)
+                ids_half = recv1[i, ROWS + 38 : ROWS + 39, :]
+                ids_half = jnp.where(low_row, pltpu.roll(ids_half, 64, 1), ids_half)
+                ident = jnp.concatenate([recv1[i, 78:79, :], ids_half], axis=1)
+                here = block == (part + source) % 4
+                values = value if source == 0 else jnp.where(here, value, values)
+                ids = ident if source == 0 else jnp.where(here, ident, ids)
+            place = base + ids.astype(jnp.int32)
+            high = values.astype(BF16)
+            rest = values - high.astype(F32)
+            middle = rest.astype(BF16)
+            tail = (rest - middle.astype(F32)).astype(BF16)
+            pieces = jnp.concatenate([high, middle, tail], axis=0)
             choice = jnp.where(wanted == place, 1.0, 0.0).astype(BF16)
             found = lax.dot_general(
                 pieces, choice, (((1,), (1,)), ((), ())), preferred_element_type=F32
             )
             found = found[0:ROWS] + found[ROWS : 2 * ROWS] + found[2 * ROWS : 3 * ROWS]
-            yield part, found
-
-    for part, found in gather(0):
-        dense[2 * part] = found[:, 0:128]
-        dense[2 * part + 1] = found[:, 128:256]
-
-    def absorb(i, carry):
+            for side in range(2):
+                piece = found[:, side * 128 : side * 128 + 128]
+                if begin:
+                    piece = dense[2 * part + side] + piece
+                dense[2 * part + side] = piece
+
+    for i in (1, 2, 3):
         copy1(i).wait_recv()
-        for part, found in gather(i):
-            dense[2 * part] = dense[2 * part] + found[:, 0:128]
-            dense[2 * part + 1] = dense[2 * part + 1] + found[:, 128:256]
-        return carry
-
-    lax.fori_loop(1, 8, absorb, 0)
+    batch(0)
+    for i in (6, 7, 4, 5):
+        copy1(i).wait_recv()
+    batch(4)
 
     def copy2(i):
         return pltpu.make_async_remote_copy(
@@ -300,12 +329,18 @@
 
 def shards(factors, dest_device, dest_node, live_count, shift):
     vmem = pl.BlockSpec(memory_space=pltpu.VMEM)
+    in_hbm = functools.partial(pltpu.with_memory_space_constraint, memory_space=pltpu.HBM)
     sums = pl.pallas_call(
         exchange_kernel,
         out_shape=jax.ShapeDtypeStruct((16, 128), F32),
-        in_specs=[vmem, vmem, vmem, pl.BlockSpec(memory_space=pltpu.SMEM)],
+        in_specs=[pl.BlockSpec(memory_space=pltpu.HBM)] * 3
+        + [pl.BlockSpec(memory_space=pltpu.SMEM)],
         out_specs=vmem,
         scratch_shapes=[
+            pltpu.VMEM((SIZE, SIZE, COUNT), BF16),
+            pltpu.VMEM((1, COUNT), jnp.int32),
+            pltpu.VMEM((1, COUNT), jnp.int32),
+            pltpu.SemaphoreType.DMA((3,)),
             pltpu.VMEM((208, COUNT), BF16),
             pltpu.VMEM((3, 208, 128), F32),
             pltpu.VMEM((3, ROWS, 128), F32),
@@ -317,14 +352,22 @@
             pltpu.VMEM((8, 16, 128), F32),
         ]
         + [pltpu.SemaphoreType.DMA((8,))] * 6,
-        compiler_params=pltpu.CompilerParams(collective_id=0, has_side_effects=True),
-    )(factors, dest_device.reshape(1, COUNT), dest_node.reshape(1, COUNT), live_count)
+        compiler_params=pltpu.CompilerParams(
+            collective_id=0, has_side_effects=True, vmem_limit_bytes=16 << 20
+        ),
+    )(
+        in_hbm(factors),
+        in_hbm(dest_device.reshape(1, COUNT)),
+        in_hbm(dest_node.reshape(1, COUNT)),
+        live_count,
+    )
     return pl.pallas_call(
         inverse_kernel,
         out_shape=jax.ShapeDtypeStruct((SIZE, SIZE, NODES), F32),
         in_specs=[vmem, vmem],
         out_specs=vmem,
         scratch_shapes=[pltpu.VMEM((ROWS, 128), F32), pltpu.VMEM((SIZE, SIZE, NODES), F32)],
+        compiler_params=pltpu.CompilerParams(vmem_limit_bytes=4 << 20),
     )(sums, shift)
 
 

time: 39.2 us -> 35.9 us (0.916)
  Pallas kernels: 38.3 us -> 35 us
    pallas_call x1, Pallas kernels: 36.7 us -> 34.1 us  [shards(): pl.pallas_call(exchange_kernel, out_shape=jax.ShapeDtypeStruct((16, 128),...]
    pallas_call x1, Pallas kernels: 1.62 us -> 0.9 us  [shards(): pl.pallas_call(inverse_kernel, out_shape=jax.ShapeDtypeStruct((SIZE, SIZE...]
where the time goes in v2:
time: 35.9 us; the launch traced here: 35.7 us
  Pallas kernels  35 us (97%)
  between operations  0.68 us (2%)
    pallas_call x1, Pallas kernels, shards(): pl.pallas_call(exchange_kernel, out_shape=jax.ShapeDtypeStruct((16, 128),...  34.1 us
    pallas_call x1, Pallas kernels, shards(): pl.pallas_call(inverse_kernel, out_shape=jax.ShapeDtypeStruct((SIZE, SIZE...  0.9 us

profile of v2, /device:TPU:1, one launch (start us, length us, event | category | flops | bytes accessed | tf_op | source)
XLA Modules:
  0.0 35.7 jit_solution(11165411463323482518)
XLA Ops:
  0.7 0.0 copy-start
  0.7 34.1 %shard_map.55.sums = f32[16,128]{1,0:T(8,128)S(1)} custom-call(bf16[12,12,1024]{2,1,0:T(8,128)(2,1)} %factors_in.1, s32[1,1024]{1,0:T(1,128)} %bitcast.2, s32[1,1024]{1,0:T(1,128)} %bitcast.3, s32[1]{0:T(128)S(6)} %copy.6.live_ref), custom_call_target="tpu_custom_call" | custom-call | tf_op jit(solution)/shard_map/pallas_call | solution.py:333
  34.8 0.0 copy-done
  34.8 0.9 %shard_map.56 = f32[12,12,16]{2,1,0:T(8,128)} custom-call(f32[16,128]{1,0:T(8,128)S(1)} %shard_map.55.sums, f32[12,16]{1,0:T(8,128)S(1)} %copy-done), custom_call_target="tpu_custom_call" | custom-call | tf_op jit(solution)/shard_map/pallas_call | solution.py:364
Async XLA Ops:
  0.7 34.1 %copy-start = (f32[12,16]{1,0:T(8,128)S(1)}, f32[12,16]{1,0:T(8,128)}, u32[]{:S(2)}) copy-start(f32[12,16]{1,0:T(8,128)} %shift.1) | copy-start | bytes 2308

commit v3 on v2

--- a/solution.py
+++ b/solution.py
@@ -122,29 +122,28 @@
 
     low = lanes((40, 128)) < 64
 
-    def prepare(step):
+    def route(step, slot_at):
         wanted = lax.broadcasted_iota(jnp.int32, (384, COUNT), 0)
         choice = jnp.where(wanted == slot - step * 384, 1.0, 0.0).astype(BF16)
         result = lax.dot_general(
             lhs[...], choice, (((1,), (1,)), ((), ())), preferred_element_type=F32
         )
         for t in range(3):
-            routed[t] = result[:, t * 128 : (t + 1) * 128]
-
-        def product(t, carry):
+            routed[slot_at * 3 + t] = result[:, t * 128 : (t + 1) * 128]
+
+    def multiply(slot_at):
+        for t in range(3):
+            source = slot_at * 3 + t
             total = [None] * SIZE
             for k in range(SIZE):
-                column = routed[t, pl.ds(k, SIZE, stride=16), :]
+                column = routed[source, pl.ds(k, SIZE, stride=16), :]
                 for a in range(SIZE):
-                    term = routed[t, a * 16 + k : a * 16 + k + 1, :] * column
+                    term = routed[source, a * 16 + k : a * 16 + k + 1, :] * column
                     total[a] = term if k == 0 else total[a] + term
             for a in range(SIZE):
-                packed[t, OFFSET[a] : OFFSET[a] + SIZE - a, :] = total[a][a:SIZE]
-            packed[t, 78:80, :] = routed[t, 192:194, :]
-            return carry
-
-        lax.fori_loop(0, 3, product, 0)
-        upper, bottom = packed[2, 0:40, :], packed[2, 40:80, :]
+                packed[source, OFFSET[a] : OFFSET[a] + SIZE - a, :] = total[a][a:SIZE]
+            packed[source, 78:80, :] = routed[source, 192:194, :]
+        upper, bottom = packed[slot_at * 3 + 2, 0:40, :], packed[slot_at * 3 + 2, 40:80, :]
         first_half = jnp.where(low, upper, pltpu.roll(bottom, 64, 1))
         second_half = jnp.where(low, pltpu.roll(upper, 64, 1), bottom)
         return first_half, second_half
@@ -163,38 +162,38 @@
             device_id_type=MESH,
         )
 
-    def send(step):
-        first_half, second_half = prepare(step)
-        fill(send1, 2 * step, 0, first_half)
-        fill(send1, 2 * step + 1, 1, second_half)
+    def pair(step, slot_at):
+        first_half, second_half = multiply(slot_at)
+        fill(recv1 if step == 0 else send1, 2 * step, slot_at * 3, first_half)
+        fill(send1, 2 * step + 1, slot_at * 3 + 1, second_half)
 
     def start(step):
-        copy1(2 * step).start()
+        if step:
+            copy1(2 * step).start()
         copy1(2 * step + 1).start()
 
-    send(2)
+    route(1, 0)
+    pair(1, 0)
+    route(3, 1)
     pl.semaphore_wait(barrier, 21)
+    start(1)
+    pair(3, 1)
+    route(2, 0)
+    start(3)
+    pair(2, 0)
+    route(0, 1)
     start(2)
-
-    def pair(turn, carry):
-        step = 1 + 2 * turn
-        send(step)
-        start(step)
-        return carry
-
-    lax.fori_loop(0, 2, pair, 0)
-    first_half, second_half = prepare(0)
-    fill(send1, 1, 1, second_half)
-    copy1(1).start()
-    fill(recv1, 0, 0, first_half)
+    pair(0, 1)
+    start(0)
 
     base = (lanes((1, 256)) & 15) * 16
     block = (lanes((1, 256)) & 63) >> 4
     low_row = lanes((1, 128)) < 64
     wanted = lax.broadcasted_iota(jnp.int32, (256, 256), 0)
 
-    def batch(begin):
-        for part in range(4):
+    def batch(begin, finish):
+        for delta in (2, 1, 3, 0):
+            part = lax.rem(first // 2 + delta, 4)
             values = ids = None
             for source in range(4):
                 i = begin + source
@@ -206,7 +205,7 @@
                 ids_half = recv1[i, ROWS + 38 : ROWS + 39, :]
                 ids_half = jnp.where(low_row, pltpu.roll(ids_half, 64, 1), ids_half)
                 ident = jnp.concatenate([recv1[i, 78:79, :], ids_half], axis=1)
-                here = block == (part + source) % 4
+                here = block == lax.rem(part + source, 4)
                 values = value if source == 0 else jnp.where(here, value, values)
                 ids = ident if source == 0 else jnp.where(here, ident, ids)
             place = base + ids.astype(jnp.int32)
@@ -225,30 +224,46 @@
                 if begin:
                     piece = dense[2 * part + side] + piece
                 dense[2 * part + side] = piece
+            finish(delta)
+
+    def copy2(target, source):
+        return pltpu.make_async_remote_copy(
+            src_ref=dense.at[target],
+            dst_ref=recv2.at[source],
+            send_sem=ssem2.at[target],
+            recv_sem=rsem2.at[source],
+            device_id=device(
+                target * (1 - core) + y * core, x, core, z * (1 - core) + target * core
+            ),
+            device_id_type=MESH,
+        )
+
+    def ship(delta):
+        part = lax.rem(first // 2 + delta, 4)
+        copy2(2 * part, first).start()
+        copy2(2 * part + 1, first).start()
+
+    def after(delta):
+        if delta == 1:
+            ship(2)
+        elif delta == 3:
+            ship(1)
+        elif delta == 0:
+            ship(3)
+            copy2(first + 1 - 2 * lax.rem(first, 2), first).start()
 
     for i in (1, 2, 3):
         copy1(i).wait_recv()
-    batch(0)
+    batch(0, lambda delta: None)
     for i in (6, 7, 4, 5):
         copy1(i).wait_recv()
-    batch(4)
-
-    def copy2(i):
-        return pltpu.make_async_remote_copy(
-            src_ref=dense.at[lax.rem(first + i, 8)],
-            dst_ref=recv2.at[i],
-            send_sem=ssem2.at[i],
-            recv_sem=rsem2.at[i],
-            device_id=partner2(i),
-            device_id_type=MESH,
-        )
-
-    for i in (4, 3, 5, 2, 6, 1, 7):
-        copy2(i).start()
+    batch(4, after)
+
     total = dense[first]
     for i in (1, 7, 2, 6, 3, 5, 4):
-        copy2(i).wait_recv()
-        total = total + recv2[i]
+        source = lax.rem(first + i, 8)
+        copy2(source, source).wait_recv()
+        total = total + recv2[source]
 
     lane_full = lanes((8, 128))
 
@@ -293,7 +308,7 @@
     out[...] = result
     for i in range(1, 8):
         copy1(i).wait_send()
-        copy2(i).wait_send()
+        copy2(lax.rem(first + i, 8), first).wait_send()
         copy3(i).wait_send()
 
 
@@ -342,8 +357,8 @@
             pltpu.VMEM((1, COUNT), jnp.int32),
             pltpu.SemaphoreType.DMA((3,)),
             pltpu.VMEM((208, COUNT), BF16),
-            pltpu.VMEM((3, 208, 128), F32),
-            pltpu.VMEM((3, ROWS, 128), F32),
+            pltpu.VMEM((6, 208, 128), F32),
+            pltpu.VMEM((6, ROWS, 128), F32),
             pltpu.VMEM((8, MESSAGE, 128), F32),
             pltpu.VMEM((8, MESSAGE, 128), F32),
             pltpu.VMEM((8, ROWS, 128), F32),

time: 35.9 us -> 34.9 us (0.972)
  Pallas kernels: 35 us -> 34 us
    pallas_call x1, Pallas kernels: 34.1 us -> 33.1 us  [shards(): pl.pallas_call(exchange_kernel, out_shape=jax.ShapeDtypeStruct((16, 128),...]
where the time goes in v3:
time: 34.9 us; the launch traced here: 34.7 us
  Pallas kernels  34 us (97%)
  between operations  0.68 us (2%)
    pallas_call x1, Pallas kernels, shards(): pl.pallas_call(exchange_kernel, out_shape=jax.ShapeDtypeStruct((16, 128),...  33.1 us
    pallas_call x1, Pallas kernels, shards(): pl.pallas_call(inverse_kernel, out_shape=jax.ShapeDtypeStruct((SIZE, SIZE...  0.9 us

profile of v3, /device:TPU:1, one launch (start us, length us, event | category | flops | bytes accessed | tf_op | source)
XLA Modules:
  0.0 34.7 jit_solution(18067177310757490768)
XLA Ops:
  0.7 0.0 copy-start
  0.7 33.1 %shard_map.55.sums = f32[16,128]{1,0:T(8,128)S(1)} custom-call(bf16[12,12,1024]{2,1,0:T(8,128)(2,1)} %factors_in.1, s32[1,1024]{1,0:T(1,128)} %bitcast.2, s32[1,1024]{1,0:T(1,128)} %bitcast.3, s32[1]{0:T(128)S(6)} %copy.6.live_ref), custom_call_target="tpu_custom_call" | custom-call | tf_op jit(solution)/shard_map/pallas_call | solution.py:348
  33.8 0.0 copy-done
  33.8 0.9 %shard_map.56 = f32[12,12,16]{2,1,0:T(8,128)} custom-call(f32[16,128]{1,0:T(8,128)S(1)} %shard_map.55.sums, f32[12,16]{1,0:T(8,128)S(1)} %copy-done), custom_call_target="tpu_custom_call" | custom-call | tf_op jit(solution)/shard_map/pallas_call | solution.py:379
Async XLA Ops:
  0.7 33.2 %copy-start = (f32[12,16]{1,0:T(8,128)S(1)}, f32[12,16]{1,0:T(8,128)}, u32[]{:S(2)}) copy-start(f32[12,16]{1,0:T(8,128)} %shift.1) | copy-start | bytes 2308

commit v4 on v3

--- a/solution.py
+++ b/solution.py
@@ -36,6 +36,11 @@
             hits = jnp.where(same, 1.0, 0.0)
             counts[later] = counts[later] + jnp.sum(hits.reshape(16, 8, 128), axis=0)
     return jnp.concatenate([jnp.sum(c, axis=0, keepdims=True) for c in counts], axis=1)
+
+
+def wait_for(buffer, begin, count, semaphore):
+    span = buffer.at[pl.ds(begin, count)]
+    pltpu.make_async_copy(span, span, semaphore).wait()
 
 
 def exchange_kernel(
@@ -57,12 +62,10 @@
     recv2,
     send3,
     recv3,
-    ssem1,
-    rsem1,
-    ssem2,
-    rsem2,
-    ssem3,
-    rsem3,
+    sent,
+    arrived,
+    ready,
+    all_ready,
 ):
     inputs = [
         pltpu.make_async_copy(source, target, isem.at[n])
@@ -91,9 +94,10 @@
         return device(lax.rem(y + i * core, NY), x, core, lax.rem(z + i * (1 - core), NZ))
 
     barrier = pltpu.get_barrier_semaphore()
-    for partner in (partner1, partner2, partner3):
-        for i in range(1, 8):
-            pl.semaphore_signal(barrier, inc=1, device_id=partner(i), device_id_type=MESH)
+    near = [partner(i) for partner in (partner2, partner3) for i in (1, 7)]
+    next_near = [partner(i) for partner in (partner2, partner3) for i in (2, 6)]
+    for target in near + [partner1(i) for i in range(1, 8)]:
+        pl.semaphore_signal(barrier, inc=1, device_id=target, device_id_type=MESH)
 
     first = y * (1 - core) + z * core
     second = z * (1 - core) + y * core
@@ -156,8 +160,8 @@
         return pltpu.make_async_remote_copy(
             src_ref=send1.at[i],
             dst_ref=recv1.at[i],
-            send_sem=ssem1.at[i],
-            recv_sem=rsem1.at[i],
+            send_sem=sent.at[0],
+            recv_sem=arrived.at[i // 4],
             device_id=partner1(i),
             device_id_type=MESH,
         )
@@ -175,8 +179,10 @@
     route(1, 0)
     pair(1, 0)
     route(3, 1)
-    pl.semaphore_wait(barrier, 21)
+    pl.semaphore_wait(barrier, 11)
     start(1)
+    for target in near:
+        pl.semaphore_signal(ready, inc=1, device_id=target, device_id_type=MESH)
     pair(3, 1)
     route(2, 0)
     start(3)
@@ -185,6 +191,9 @@
     start(2)
     pair(0, 1)
     start(0)
+    pl.semaphore_wait(ready, 4)
+    for target in next_near:
+        pl.semaphore_signal(all_ready, inc=1, device_id=target, device_id_type=MESH)
 
     base = (lanes((1, 256)) & 15) * 16
     block = (lanes((1, 256)) & 63) >> 4
@@ -230,8 +239,8 @@
         return pltpu.make_async_remote_copy(
             src_ref=dense.at[target],
             dst_ref=recv2.at[source],
-            send_sem=ssem2.at[target],
-            recv_sem=rsem2.at[source],
+            send_sem=sent.at[1],
+            recv_sem=arrived.at[2],
             device_id=device(
                 target * (1 - core) + y * core, x, core, z * (1 - core) + target * core
             ),
@@ -244,26 +253,21 @@
         copy2(2 * part + 1, first).start()
 
     def after(delta):
-        if delta == 1:
-            ship(2)
-        elif delta == 3:
-            ship(1)
-        elif delta == 0:
-            ship(3)
+        if delta:
+            ship(delta)
+        else:
             copy2(first + 1 - 2 * lax.rem(first, 2), first).start()
 
-    for i in (1, 2, 3):
-        copy1(i).wait_recv()
+    wait_for(recv1, 1, 3, arrived.at[0])
     batch(0, lambda delta: None)
-    for i in (6, 7, 4, 5):
-        copy1(i).wait_recv()
+    wait_for(recv1, 4, 4, arrived.at[1])
+    pl.semaphore_wait(all_ready, 4)
     batch(4, after)
 
     total = dense[first]
-    for i in (1, 7, 2, 6, 3, 5, 4):
-        source = lax.rem(first + i, 8)
-        copy2(source, source).wait_recv()
-        total = total + recv2[source]
+    wait_for(recv2, 0, 7, arrived.at[2])
+    for i in range(1, 8):
+        total = total + recv2[lax.rem(first + i, 8)]
 
     lane_full = lanes((8, 128))
 
@@ -293,8 +297,8 @@
         return pltpu.make_async_remote_copy(
             src_ref=send3.at[lax.rem(second + i, 8)],
             dst_ref=recv3.at[i],
-            send_sem=ssem3.at[i],
-            recv_sem=rsem3.at[i],
+            send_sem=sent.at[2],
+            recv_sem=arrived.at[3],
             device_id=partner3(i),
             device_id_type=MESH,
         )
@@ -302,14 +306,13 @@
     for i in (4, 3, 5, 2, 6, 1, 7):
         copy3(i).start()
     result = send3[second]
-    for i in (1, 7, 2, 6, 3, 5, 4):
-        copy3(i).wait_recv()
+    wait_for(recv3, 1, 7, arrived.at[3])
+    for i in range(1, 8):
         result = result + recv3[i]
     out[...] = result
-    for i in range(1, 8):
-        copy1(i).wait_send()
-        copy2(lax.rem(first + i, 8), first).wait_send()
-        copy3(i).wait_send()
+    wait_for(recv1, 1, 7, sent.at[0])
+    wait_for(recv2, 0, 7, sent.at[1])
+    wait_for(recv3, 1, 7, sent.at[2])
 
 
 def inverse_kernel(sums, shift, out, flat, square):
@@ -366,7 +369,8 @@
             pltpu.VMEM((8, 16, 128), F32),
             pltpu.VMEM((8, 16, 128), F32),
         ]
-        + [pltpu.SemaphoreType.DMA((8,))] * 6,
+        + [pltpu.SemaphoreType.DMA((3,)), pltpu.SemaphoreType.DMA((4,))]
+        + [pltpu.SemaphoreType.REGULAR] * 2,
         compiler_params=pltpu.CompilerParams(
             collective_id=0, has_side_effects=True, vmem_limit_bytes=16 << 20
         ),

time: 34.9 us -> 34.2 us (0.980)
  Pallas kernels: 34 us -> 33.4 us
    pallas_call x1, Pallas kernels: 33.1 us -> 32.5 us  [shards(): pl.pallas_call(exchange_kernel, out_shape=jax.ShapeDtypeStruct((16, 128),...]
where the time goes in v4:
time: 34.2 us; the launch traced here: 34.1 us
  Pallas kernels  33.4 us (98%)
  between operations  0.68 us (2%)
    pallas_call x1, Pallas kernels, shards(): pl.pallas_call(exchange_kernel, out_shape=jax.ShapeDtypeStruct((16, 128),...  32.5 us
    pallas_call x1, Pallas kernels, shards(): pl.pallas_call(inverse_kernel, out_shape=jax.ShapeDtypeStruct((SIZE, SIZE...  0.9 us

profile of v4, /device:TPU:1, one launch (start us, length us, event | category | flops | bytes accessed | tf_op | source)
XLA Modules:
  0.0 34.1 jit_solution(1105424108548785137)
XLA Ops:
  0.7 0.0 copy-start
  0.7 32.5 %shard_map.55.sums = f32[16,128]{1,0:T(8,128)S(1)} custom-call(bf16[12,12,1024]{2,1,0:T(8,128)(2,1)} %factors_in.1, s32[1,1024]{1,0:T(1,128)} %bitcast.2, s32[1,1024]{1,0:T(1,128)} %bitcast.3, s32[1]{0:T(128)S(6)} %copy.6.live_ref), custom_call_target="tpu_custom_call" | custom-call | tf_op jit(solution)/shard_map/pallas_call | solution.py:351
  33.2 0.0 copy-done
  33.2 0.9 %shard_map.56 = f32[12,12,16]{2,1,0:T(8,128)} custom-call(f32[16,128]{1,0:T(8,128)S(1)} %shard_map.55.sums, f32[12,16]{1,0:T(8,128)S(1)} %copy-done), custom_call_target="tpu_custom_call" | custom-call | tf_op jit(solution)/shard_map/pallas_call | solution.py:383
Async XLA Ops:
  0.7 32.5 %copy-start = (f32[12,16]{1,0:T(8,128)S(1)}, f32[12,16]{1,0:T(8,128)}, u32[]{:S(2)}) copy-start(f32[12,16]{1,0:T(8,128)} %shift.1) | copy-start | bytes 2308

commit v5 on v4

--- a/solution.py
+++ b/solution.py
@@ -14,9 +14,10 @@
 COUNT = 1024
 NODES = 16
 NX, NY, NZ, NC = 4, 8, 8, 2
-OFFSET = [a * SIZE - a * (a - 1) // 2 for a in range(SIZE)]
+OFFSET = [1 + a * SIZE - a * (a - 1) // 2 for a in range(SIZE)]
 ROWS = 80
 MESSAGE = 120
+CHUNKS = ((0, 48), (48, 32))
 
 
 def lanes(shape):
@@ -38,8 +39,10 @@
     return jnp.concatenate([jnp.sum(c, axis=0, keepdims=True) for c in counts], axis=1)
 
 
-def wait_for(buffer, begin, count, semaphore):
+def wait_for(buffer, begin, count, semaphore, rows=None):
     span = buffer.at[pl.ds(begin, count)]
+    if rows is not None:
+        span = buffer.at[pl.ds(begin, count), pl.ds(*rows)]
     pltpu.make_async_copy(span, span, semaphore).wait()
 
 
@@ -124,8 +127,6 @@
         lhs[a * 16 : a * 16 + SIZE, :] = factors[a]
     lhs[192:208, :] = jnp.broadcast_to(node_ref[...].astype(F32), (16, COUNT)).astype(BF16)
 
-    low = lanes((40, 128)) < 64
-
     def route(step, slot_at):
         wanted = lax.broadcasted_iota(jnp.int32, (384, COUNT), 0)
         choice = jnp.where(wanted == slot - step * 384, 1.0, 0.0).astype(BF16)
@@ -146,51 +147,62 @@
                     total[a] = term if k == 0 else total[a] + term
             for a in range(SIZE):
                 packed[source, OFFSET[a] : OFFSET[a] + SIZE - a, :] = total[a][a:SIZE]
-            packed[source, 78:80, :] = routed[source, 192:194, :]
-        upper, bottom = packed[slot_at * 3 + 2, 0:40, :], packed[slot_at * 3 + 2, 40:80, :]
-        first_half = jnp.where(low, upper, pltpu.roll(bottom, 64, 1))
-        second_half = jnp.where(low, pltpu.roll(upper, 64, 1), bottom)
-        return first_half, second_half
-
-    def fill(target, index, part, half):
-        target[index, 0:ROWS, :] = packed[part]
-        target[index, ROWS:MESSAGE, :] = half
-
-    def copy1(i):
+            packed[source, 0:1, :] = routed[source, 192:193, :]
+            packed[source, 79:80, :] = routed[source, 192:193, :]
+
+    def fill(target, index, part, tail):
+        for begin, rows in CHUNKS:
+            place = begin * 3 // 2
+            target[index, place : place + rows, :] = packed[part, begin : begin + rows, :]
+            half = rows // 2
+            upper = packed[tail, begin : begin + half, :]
+            bottom = packed[tail, begin + half : begin + rows, :]
+            low = lanes((half, 128)) < 64
+            if part == tail - 2:
+                both = jnp.where(low, upper, pltpu.roll(bottom, 64, 1))
+            else:
+                both = jnp.where(low, pltpu.roll(upper, 64, 1), bottom)
+            target[index, place + rows : place + rows + half, :] = both
+
+    def copy1(i, chunk):
+        begin, rows = CHUNKS[chunk]
+        span = pl.ds(begin * 3 // 2, rows * 3 // 2)
         return pltpu.make_async_remote_copy(
-            src_ref=send1.at[i],
-            dst_ref=recv1.at[i],
+            src_ref=send1.at[i, span],
+            dst_ref=recv1.at[i, span],
             send_sem=sent.at[0],
-            recv_sem=arrived.at[i // 4],
+            recv_sem=arrived.at[chunk * 2 + i // 4],
             device_id=partner1(i),
             device_id_type=MESH,
         )
 
     def pair(step, slot_at):
-        first_half, second_half = multiply(slot_at)
-        fill(recv1 if step == 0 else send1, 2 * step, slot_at * 3, first_half)
-        fill(send1, 2 * step + 1, slot_at * 3 + 1, second_half)
-
-    def start(step):
+        multiply(slot_at)
+        fill(recv1 if step == 0 else send1, 2 * step, slot_at * 3, slot_at * 3 + 2)
+        fill(send1, 2 * step + 1, slot_at * 3 + 1, slot_at * 3 + 2)
+
+    def start(step, chunk):
         if step:
-            copy1(2 * step).start()
-        copy1(2 * step + 1).start()
+            copy1(2 * step, chunk).start()
+        copy1(2 * step + 1, chunk).start()
 
     route(1, 0)
     pair(1, 0)
     route(3, 1)
     pl.semaphore_wait(barrier, 11)
-    start(1)
+    start(1, 0)
     for target in near:
         pl.semaphore_signal(ready, inc=1, device_id=target, device_id_type=MESH)
     pair(3, 1)
     route(2, 0)
-    start(3)
+    start(3, 0)
     pair(2, 0)
     route(0, 1)
-    start(2)
+    start(2, 0)
     pair(0, 1)
-    start(0)
+    start(0, 0)
+    for step in (1, 3, 2, 0):
+        start(step, 1)
     pl.semaphore_wait(ready, 4)
     for target in next_near:
         pl.semaphore_signal(all_ready, inc=1, device_id=target, device_id_type=MESH)
@@ -200,20 +212,23 @@
     low_row = lanes((1, 128)) < 64
     wanted = lax.broadcasted_iota(jnp.int32, (256, 256), 0)
 
-    def batch(begin, finish):
+    def batch(begin, chunk):
+        first_row, rows = CHUNKS[chunk]
+        at = first_row * 3 // 2
+        low = lanes((rows // 2, 128)) < 64
         for delta in (2, 1, 3, 0):
             part = lax.rem(first // 2 + delta, 4)
             values = ids = None
             for source in range(4):
                 i = begin + source
-                half = recv1[i, ROWS:MESSAGE, :]
+                half = recv1[i, at + rows : at + rows * 3 // 2, :]
                 spread = jnp.concatenate(
                     [jnp.where(low, half, 0.0), jnp.where(low, 0.0, half)], axis=0
                 )
-                value = jnp.concatenate([recv1[i, 0:ROWS, :], spread], axis=1)
-                ids_half = recv1[i, ROWS + 38 : ROWS + 39, :]
-                ids_half = jnp.where(low_row, pltpu.roll(ids_half, 64, 1), ids_half)
-                ident = jnp.concatenate([recv1[i, 78:79, :], ids_half], axis=1)
+                value = jnp.concatenate([recv1[i, at : at + rows, :], spread], axis=1)
+                ids_half = recv1[i, 48:49, :]
+                ids_half = jnp.where(low_row, ids_half, pltpu.roll(ids_half, 64, 1))
+                ident = jnp.concatenate([recv1[i, 0:1, :], ids_half], axis=1)
                 here = block == lax.rem(part + source, 4)
                 values = value if source == 0 else jnp.where(here, value, values)
                 ids = ident if source == 0 else jnp.where(here, ident, ids)
@@ -227,47 +242,39 @@
             found = lax.dot_general(
                 pieces, choice, (((1,), (1,)), ((), ())), preferred_element_type=F32
             )
-            found = found[0:ROWS] + found[ROWS : 2 * ROWS] + found[2 * ROWS : 3 * ROWS]
+            found = found[0:rows] + found[rows : 2 * rows] + found[2 * rows : 3 * rows]
             for side in range(2):
                 piece = found[:, side * 128 : side * 128 + 128]
                 if begin:
-                    piece = dense[2 * part + side] + piece
-                dense[2 * part + side] = piece
-            finish(delta)
-
-    def copy2(target, source):
+                    piece = dense[2 * part + side, first_row : first_row + rows, :] + piece
+                dense[2 * part + side, first_row : first_row + rows, :] = piece
+            if begin and delta:
+                copy2(2 * part, first, chunk).start()
+                copy2(2 * part + 1, first, chunk).start()
+            elif begin:
+                copy2(first + 1 - 2 * lax.rem(first, 2), first, chunk).start()
+
+    def copy2(target, source, chunk):
+        begin, rows = CHUNKS[chunk]
         return pltpu.make_async_remote_copy(
-            src_ref=dense.at[target],
-            dst_ref=recv2.at[source],
+            src_ref=dense.at[target, pl.ds(begin, rows)],
+            dst_ref=recv2.at[source, pl.ds(begin, rows)],
             send_sem=sent.at[1],
-            recv_sem=arrived.at[2],
+            recv_sem=arrived.at[4 + chunk],
             device_id=device(
                 target * (1 - core) + y * core, x, core, z * (1 - core) + target * core
             ),
             device_id_type=MESH,
         )
 
-    def ship(delta):
-        part = lax.rem(first // 2 + delta, 4)
-        copy2(2 * part, first).start()
-        copy2(2 * part + 1, first).start()
-
-    def after(delta):
-        if delta:
-            ship(delta)
-        else:
-            copy2(first + 1 - 2 * lax.rem(first, 2), first).start()
-
-    wait_for(recv1, 1, 3, arrived.at[0])
-    batch(0, lambda delta: None)
-    wait_for(recv1, 4, 4, arrived.at[1])
-    pl.semaphore_wait(all_ready, 4)
-    batch(4, after)
-
-    total = dense[first]
-    wait_for(recv2, 0, 7, arrived.at[2])
-    for i in range(1, 8):
-        total = total + recv2[lax.rem(first + i, 8)]
+    for chunk, (begin, rows) in enumerate(CHUNKS):
+        part_rows = (begin * 3 // 2, rows * 3 // 2)
+        wait_for(recv1, 1, 3, arrived.at[chunk * 2], part_rows)
+        batch(0, chunk)
+        wait_for(recv1, 4, 4, arrived.at[chunk * 2 + 1], part_rows)
+        if chunk == 0:
+            pl.semaphore_wait(all_ready, 4)
+        batch(4, chunk)
 
     lane_full = lanes((8, 128))
 
@@ -285,31 +292,34 @@
             tiles = result
         return tiles
 
-    rows = [total[v * 8 : v * 8 + 8] for v in range(10)]
-    empty = jnp.zeros((8, 128), F32)
-    main = swap(rows[0:8])
-    extra = swap(rows[8:10] + [empty] * 6)
-    for q in range(8):
-        send3[q, 0:8, :] = main[q]
-        send3[q, 8:16, :] = extra[q]
-
-    def copy3(i):
+    def copy3(i, chunk):
         return pltpu.make_async_remote_copy(
-            src_ref=send3.at[lax.rem(second + i, 8)],
-            dst_ref=recv3.at[i],
+            src_ref=send3.at[lax.rem(second + i, 8), chunk],
+            dst_ref=recv3.at[i, chunk],
             send_sem=sent.at[2],
-            recv_sem=arrived.at[3],
+            recv_sem=arrived.at[6],
             device_id=partner3(i),
             device_id_type=MESH,
         )
 
-    for i in (4, 3, 5, 2, 6, 1, 7):
-        copy3(i).start()
-    result = send3[second]
-    wait_for(recv3, 1, 7, arrived.at[3])
-    for i in range(1, 8):
-        result = result + recv3[i]
-    out[...] = result
+    empty = jnp.zeros((8, 128), F32)
+    for chunk, (begin, rows) in enumerate(CHUNKS):
+        wait_for(recv2, 0, 7, arrived.at[4 + chunk], (begin, rows))
+        total = dense[first, begin : begin + rows, :]
+        for i in range(1, 8):
+            total = total + recv2[lax.rem(first + i, 8), begin : begin + rows, :]
+        tiles = [total[v * 8 : v * 8 + 8] for v in range(rows // 8)]
+        tiles = swap(tiles + [empty] * (8 - len(tiles)))
+        for q in range(8):
+            send3[q, chunk] = tiles[q]
+        for i in (4, 3, 5, 2, 6, 1, 7):
+            copy3(i, chunk).start()
+    wait_for(recv3, 1, 7, arrived.at[6])
+    for chunk in range(2):
+        result = send3[second, chunk]
+        for i in range(1, 8):
+            result = result + recv3[i, chunk]
+        out[chunk * 8 : chunk * 8 + 8, :] = result
     wait_for(recv1, 1, 7, sent.at[0])
     wait_for(recv2, 0, 7, sent.at[1])
     wait_for(recv3, 1, 7, sent.at[2])
@@ -317,8 +327,8 @@
 
 def inverse_kernel(sums, shift, out, flat, square):
     for v in range(10):
-        source = sums[0:8, :] if v < 8 else sums[8:16, :]
-        turned = 16 * v % 128
+        source = sums[0:8, :] if v < 6 else sums[8:16, :]
+        turned = 16 * (v if v < 6 else v - 6)
         flat[v * 8 : v * 8 + 8, :] = pltpu.roll(source, 128 - turned, 1) if turned else source
     for j in range(SIZE):
         square[j, j:SIZE, :] = flat[OFFSET[j] : OFFSET[j] + SIZE - j, 0:NODES]
@@ -366,10 +376,10 @@
             pltpu.VMEM((8, MESSAGE, 128), F32),
             pltpu.VMEM((8, ROWS, 128), F32),
             pltpu.VMEM((8, ROWS, 128), F32),
-            pltpu.VMEM((8, 16, 128), F32),
-            pltpu.VMEM((8, 16, 128), F32),
+            pltpu.VMEM((8, 2, 8, 128), F32),
+            pltpu.VMEM((8, 2, 8, 128), F32),
         ]
-        + [pltpu.SemaphoreType.DMA((3,)), pltpu.SemaphoreType.DMA((4,))]
+        + [pltpu.SemaphoreType.DMA((3,)), pltpu.SemaphoreType.DMA((7,))]
         + [pltpu.SemaphoreType.REGULAR] * 2,
         compiler_params=pltpu.CompilerParams(
             collective_id=0, has_side_effects=True, vmem_limit_bytes=16 << 20

time: 34.2 us -> 33.2 us (0.971)
  Pallas kernels: 33.4 us -> 32.3 us
    pallas_call x1, Pallas kernels: 32.5 us -> 31.4 us  [shards(): pl.pallas_call(exchange_kernel, out_shape=jax.ShapeDtypeStruct((16, 128),...]
where the time goes in v5:
time: 33.2 us; the launch traced here: 33 us
  Pallas kernels  32.3 us (97%)
  between operations  0.68 us (2%)
    pallas_call x1, Pallas kernels, shards(): pl.pallas_call(exchange_kernel, out_shape=jax.ShapeDtypeStruct((16, 128),...  31.4 us
    pallas_call x1, Pallas kernels, shards(): pl.pallas_call(inverse_kernel, out_shape=jax.ShapeDtypeStruct((SIZE, SIZE...  0.9 us

profile of v5, /device:TPU:1, one launch (start us, length us, event | category | flops | bytes accessed | tf_op | source)
XLA Modules:
  0.0 33.0 jit_solution(7203425597695823900)
XLA Ops:
  0.7 0.0 copy-start
  0.7 31.4 %shard_map.55.sums = f32[16,128]{1,0:T(8,128)S(1)} custom-call(bf16[12,12,1024]{2,1,0:T(8,128)(2,1)} %factors_in.1, s32[1,1024]{1,0:T(1,128)} %bitcast.2, s32[1,1024]{1,0:T(1,128)} %bitcast.3, s32[1]{0:T(128)S(6)} %copy.6.live_ref), custom_call_target="tpu_custom_call" | custom-call | tf_op jit(solution)/shard_map/pallas_call | solution.py:361
  32.1 0.0 copy-done
  32.1 0.9 %shard_map.56 = f32[12,12,16]{2,1,0:T(8,128)} custom-call(f32[16,128]{1,0:T(8,128)S(1)} %shard_map.55.sums, f32[12,16]{1,0:T(8,128)S(1)} %copy-done), custom_call_target="tpu_custom_call" | custom-call | tf_op jit(solution)/shard_map/pallas_call | solution.py:393
Async XLA Ops:
  0.7 31.4 %copy-start = (f32[12,16]{1,0:T(8,128)S(1)}, f32[12,16]{1,0:T(8,128)}, u32[]{:S(2)}) copy-start(f32[12,16]{1,0:T(8,128)} %shift.1) | copy-start | bytes 2308

commit v6 on v5

--- a/solution.py
+++ b/solution.py
@@ -91,10 +91,10 @@
         return device(y, lax.rem(x + i // 2, NX), lax.rem(core + i, NC), z)
 
     def partner2(i):
+        return device(lax.rem(y + i * core, NY), x, core, lax.rem(z + i * (1 - core), NZ))
+
+    def partner3(i):
         return device(lax.rem(y + i * (1 - core), NY), x, core, lax.rem(z + i * core, NZ))
-
-    def partner3(i):
-        return device(lax.rem(y + i * core, NY), x, core, lax.rem(z + i * (1 - core), NZ))
 
     barrier = pltpu.get_barrier_semaphore()
     near = [partner(i) for partner in (partner2, partner3) for i in (1, 7)]
@@ -102,8 +102,8 @@
     for target in near + [partner1(i) for i in range(1, 8)]:
         pl.semaphore_signal(barrier, inc=1, device_id=target, device_id_type=MESH)
 
-    first = y * (1 - core) + z * core
-    second = z * (1 - core) + y * core
+    first = y * core + z * (1 - core)
+    second = z * core + y * (1 - core)
 
     inputs[0].wait()
     owner = owner_ref[...]
@@ -115,8 +115,8 @@
     other = owner_core ^ core
     step = (owner_x - x + NX) & 3
     slot = jnp.where(rank < 2, other * 128 + rank * 64, 256 + other * 64)
-    outer = owner_y * (1 - owner_core) + owner_z * owner_core
-    inner = owner_z * (1 - owner_core) + owner_y * owner_core
+    outer = owner_y * owner_core + owner_z * (1 - owner_core)
+    inner = owner_z * owner_core + owner_y * (1 - owner_core)
     lane = (outer * 8 + inner + ((2 * step + other) & 3) * 16) & 63
     slot = slot + step * 384 + lane
     slot = jnp.where(lanes((1, COUNT)) < live_ref[0], slot, -1)
@@ -262,7 +262,7 @@
             send_sem=sent.at[1],
             recv_sem=arrived.at[4 + chunk],
             device_id=device(
-                target * (1 - core) + y * core, x, core, z * (1 - core) + target * core
+                target * core + y * (1 - core), x, core, z * core + target * (1 - core)
             ),
             device_id_type=MESH,
         )

time: 33.2 us -> 33 us (level)
  the two profiles are of different devices: /device:TPU:1 before, /device:TPU:2 now
where the time goes in v6:
time: 33 us; the launch traced here: 32.8 us
  Pallas kernels  32.1 us (97%)
  between operations  0.68 us (2%)
    pallas_call x1, Pallas kernels, shards(): pl.pallas_call(exchange_kernel, out_shape=jax.ShapeDtypeStruct((16, 128),...  31.2 us
    pallas_call x1, Pallas kernels, shards(): pl.pallas_call(inverse_kernel, out_shape=jax.ShapeDtypeStruct((SIZE, SIZE...  0.9 us

profile of v6, /device:TPU:2, one launch (start us, length us, event | category | flops | bytes accessed | tf_op | source)
XLA Modules:
  0.0 32.8 jit_solution(15607297218708595993)
XLA Ops:
  0.7 0.0 copy-start
  0.7 31.2 %shard_map.55.sums = f32[16,128]{1,0:T(8,128)S(1)} custom-call(bf16[12,12,1024]{2,1,0:T(8,128)(2,1)} %factors_in.1, s32[1,1024]{1,0:T(1,128)} %bitcast.2, s32[1,1024]{1,0:T(1,128)} %bitcast.3, s32[1]{0:T(128)S(6)} %copy.6.live_ref), custom_call_target="tpu_custom_call" | custom-call | tf_op jit(solution)/shard_map/pallas_call | solution.py:361
  31.9 0.0 copy-done
  31.9 0.9 %shard_map.56 = f32[12,12,16]{2,1,0:T(8,128)} custom-call(f32[16,128]{1,0:T(8,128)S(1)} %shard_map.55.sums, f32[12,16]{1,0:T(8,128)S(1)} %copy-done), custom_call_target="tpu_custom_call" | custom-call | tf_op jit(solution)/shard_map/pallas_call | solution.py:393
Async XLA Ops:
  0.7 31.3 %copy-start = (f32[12,16]{1,0:T(8,128)S(1)}, f32[12,16]{1,0:T(8,128)}, u32[]{:S(2)}) copy-start(f32[12,16]{1,0:T(8,128)} %shift.1) | copy-start | bytes 2308

commit v7 on v6

--- a/solution.py
+++ b/solution.py
@@ -197,8 +197,8 @@
     route(2, 0)
     start(3, 0)
     pair(2, 0)
+    start(2, 0)
     route(0, 1)
-    start(2, 0)
     pair(0, 1)
     start(0, 0)
     for step in (1, 3, 2, 0):

time: 33 us -> 33 us (level)
  the two profiles are of different devices: /device:TPU:2 before, /device:TPU:1 now
where the time goes in v7:
time: 33 us; the launch traced here: 32.4 us
  Pallas kernels  31.7 us (96%)
  between operations  0.68 us (2%)
    pallas_call x1, Pallas kernels, shards(): pl.pallas_call(exchange_kernel, out_shape=jax.ShapeDtypeStruct((16, 128),...  30.8 us
    pallas_call x1, Pallas kernels, shards(): pl.pallas_call(inverse_kernel, out_shape=jax.ShapeDtypeStruct((SIZE, SIZE...  0.9 us

profile of v7, /device:TPU:1, one launch (start us, length us, event | category | flops | bytes accessed | tf_op | source)
XLA Modules:
  0.0 32.4 jit_solution(3198672188058260849)
XLA Ops:
  0.7 0.0 copy-start
  0.7 30.8 %shard_map.55.sums = f32[16,128]{1,0:T(8,128)S(1)} custom-call(bf16[12,12,1024]{2,1,0:T(8,128)(2,1)} %factors_in.1, s32[1,1024]{1,0:T(1,128)} %bitcast.2, s32[1,1024]{1,0:T(1,128)} %bitcast.3, s32[1]{0:T(128)S(6)} %copy.6.live_ref), custom_call_target="tpu_custom_call" | custom-call | tf_op jit(solution)/shard_map/pallas_call | solution.py:361
  31.5 0.0 copy-done
  31.5 0.9 %shard_map.56 = f32[12,12,16]{2,1,0:T(8,128)} custom-call(f32[16,128]{1,0:T(8,128)S(1)} %shard_map.55.sums, f32[12,16]{1,0:T(8,128)S(1)} %copy-done), custom_call_target="tpu_custom_call" | custom-call | tf_op jit(solution)/shard_map/pallas_call | solution.py:393
Async XLA Ops:
  0.7 30.8 %copy-start = (f32[12,16]{1,0:T(8,128)S(1)}, f32[12,16]{1,0:T(8,128)}, u32[]{:S(2)}) copy-start(f32[12,16]{1,0:T(8,128)} %shift.1) | copy-start | bytes 2308
